TPU v7x, 32 devices: a whole 2x2x4 slice. The times are simulated.
32 devices in a mesh: expert: 8 (over z, y), tensor: 4 (over x, core).
Axes of the slice: x: 2, y: 2, z: 4, core: 2. Of those that a mesh axis runs over, the one named last changes fastest.
Arguments:
- tokens: bfloat16 [1024, 2048], P('expert', 'tensor'), may hold values from -6 to 6
- grad_out: bfloat16 [1024, 2048], P('expert', 'tensor'), may hold values from -6 to 6
- route_weights: float32 [1024, 8], P('expert'), may hold values from 0.02 to 0.5
- expert_ids: int32 [1024, 8], P('expert'), may hold values from 0 to 15, all different within a row; in each aligned block of 128 rows (0 to 127, 128 to 255, ...) at most 96 rows name the same one
- gate_weight: bfloat16 [16, 2048, 768], P('expert', None, 'tensor'), may hold values from -0.125 to 0.125
- up_weight: bfloat16 [16, 2048, 768], P('expert', None, 'tensor'), may hold values from -0.125 to 0.125
- down_weight: bfloat16 [16, 768, 2048], P('expert', 'tensor'), may hold values from -0.21875 to 0.21875
- gate_adapter_first: bfloat16 [16, 2048, 64], P('expert'), may hold values from -0.125 to 0.125
- gate_adapter_second: bfloat16 [16, 64, 768], P('expert', None, 'tensor'), may hold values from -0.75 to 0.75
- up_adapter_first: bfloat16 [16, 2048, 64], P('expert'), may hold values from -0.125 to 0.125
- up_adapter_second: bfloat16 [16, 64, 768], P('expert', None, 'tensor'), may hold values from -0.75 to 0.75
- down_adapter_first: bfloat16 [16, 768, 64], P('expert', 'tensor'), may hold values from -0.21875 to 0.21875
- down_adapter_second: bfloat16 [16, 64, 2048], P('expert'), may hold values from -0.75 to 0.75
Outputs:
- grad_tokens: bfloat16 [1024, 2048], P('expert', 'tensor')
- gate_first_gradient: float32 [16, 2048, 64], P('expert', 'tensor')
- gate_second_gradient: float32 [16, 64, 768], P('expert', None, 'tensor')
- up_first_gradient: float32 [16, 2048, 64], P('expert', 'tensor')
- up_second_gradient: float32 [16, 64, 768], P('expert', None, 'tensor')
- down_first_gradient: float32 [16, 768, 64], P('expert', 'tensor')
- down_second_gradient: float32 [16, 64, 2048], P('expert', None, 'tensor')
Inputs may be any that keep to these rules, and one draw needn't show every extreme that they name: `expert_ids`: each token names 8 different experts. Among the 128 rows of one device no expert is named more than 96 times, a bound that some block reaches.
All inputs are finite; a program needn't handle non-finite values.
Results may differ from a plain program's by a relative error of at most 0.012.
Values may be sent and summed in bfloat16 or wider, within the bound.
A program may use at most 128 MiB of HBM per device.

v0:
```python
import jax
import jax.numpy as jnp
from jax import lax
from jax.sharding import PartitionSpec as P

adapter_scale = 0.5


def slot_positions(expert_ids, experts_all, capacity):
    tok_rows = expert_ids.shape[0]
    numbers = lax.broadcasted_iota(jnp.int32, (1, 1, experts_all), 2)
    picked = jnp.sum((expert_ids[:, :, None] == numbers).astype(jnp.float32), axis=1).astype(
        jnp.bfloat16
    )
    row_index = lax.broadcasted_iota(jnp.int32, (tok_rows, tok_rows), 0)
    col_index = lax.broadcasted_iota(jnp.int32, (tok_rows, tok_rows), 1)
    earlier = (row_index > col_index).astype(jnp.bfloat16)
    before = jnp.dot(earlier, picked, preferred_element_type=jnp.float32)
    slot_index = jnp.take_along_axis(before, expert_ids, axis=1).astype(jnp.int32)
    return expert_ids * capacity + slot_index


def fill_slots(values, positions, slot_count):
    width = values.shape[-1]
    flat = values.reshape(-1, width)
    return jnp.zeros((slot_count, width), values.dtype).at[positions.reshape(-1)].set(flat)


def local(
    tokens,
    grad_out,
    route_weights,
    expert_ids,
    gate_weight,
    up_weight,
    down_weight,
    gate_adapter_first,
    gate_adapter_second,
    up_adapter_first,
    up_adapter_second,
    down_adapter_first,
    down_adapter_second,
):
    single_float = jnp.float32
    brain_float_half = jnp.bfloat16
    tok_rows, top_count = expert_ids.shape
    local_experts = gate_weight.shape[0]
    sources = lax.axis_size("expert")
    experts_all = local_experts * sources
    capacity = 3 * tok_rows * top_count // (2 * experts_all)
    slot_count = experts_all * capacity
    positions = slot_positions(expert_ids, experts_all, capacity)
    width = tokens.shape[1]
    spread_in = jnp.broadcast_to(tokens[:, None, :], (tok_rows, top_count, width))
    scaled = (route_weights[:, :, None] * grad_out[:, None, :].astype(single_float)).astype(
        brain_float_half
    )
    send_in = fill_slots(spread_in, positions, slot_count)
    send_grad = fill_slots(scaled, positions, slot_count)
    part_in, part_grad = (
        lax.all_to_all(send_in, "expert", split_axis=0, concat_axis=0, tiled=True),
        lax.all_to_all(send_grad, "expert", split_axis=0, concat_axis=0, tiled=True),
    )
    recv_in, recv_grad = (
        lax.all_gather(part_in, "tensor", axis=1, tiled=True),
        lax.all_gather(part_grad, "tensor", axis=1, tiled=True),
    )
    hidden_width = recv_in.shape[1]
    routed_input = recv_in.reshape(sources, local_experts, capacity, hidden_width)
    routed_gradient = recv_grad.reshape(sources, local_experts, capacity, hidden_width)
    slice_width = hidden_width // lax.axis_size("tensor")
    slice_start = lax.axis_index("tensor") * slice_width
    adapter_gate_term = jnp.einsum(
        "mbtk,bkz->mbtz", routed_input, gate_adapter_first, preferred_element_type=single_float
    ).astype(brain_float_half)
    adapter_up_term = jnp.einsum(
        "mbtk,bkz->mbtz", routed_input, up_adapter_first, preferred_element_type=single_float
    ).astype(brain_float_half)
    gate_activation = jnp.einsum(
        "secd,edf->secf", routed_input, gate_weight, preferred_element_type=single_float
    )
    gate_activation = gate_activation + adapter_scale * jnp.einsum(
        "imal,mlt->imat",
        adapter_gate_term,
        gate_adapter_second,
        preferred_element_type=single_float,
    )
    up_activation = jnp.einsum(
        "secd,edf->secf", routed_input, up_weight, preferred_element_type=single_float
    )
    up_activation = up_activation + adapter_scale * jnp.einsum(
        "imal,mlt->imat", adapter_up_term, up_adapter_second, preferred_element_type=single_float
    )
    sigma = jax.nn.sigmoid(gate_activation)
    active = gate_activation * sigma
    hidden_activation = (active * up_activation).astype(brain_float_half)
    down_part = jnp.einsum(
        "secf,efr->secr", hidden_activation, down_adapter_first, preferred_element_type=single_float
    )
    down_total = lax.psum(down_part.astype(jnp.bfloat16), "tensor").astype(jnp.float32)
    backward_adapter_term = jnp.einsum(
        "secd,erd->secr", routed_gradient, down_adapter_second, preferred_element_type=single_float
    ).astype(brain_float_half)
    hidden_gradient = jnp.einsum(
        "secd,efd->secf", routed_gradient, down_weight, preferred_element_type=single_float
    )
    hidden_gradient = hidden_gradient + adapter_scale * jnp.einsum(
        "oamh,ath->oamt",
        backward_adapter_term,
        down_adapter_first,
        preferred_element_type=single_float,
    )
    gate_gradient = (
        hidden_gradient * up_activation * sigma * (1.0 + gate_activation * (1.0 - sigma))
    ).astype(brain_float_half)
    upward_gradient = (hidden_gradient * active).astype(brain_float_half)
    gate_part = jnp.einsum(
        "secf,erf->secr", gate_gradient, gate_adapter_second, preferred_element_type=single_float
    )
    up_part = jnp.einsum(
        "secf,erf->secr", upward_gradient, up_adapter_second, preferred_element_type=single_float
    )
    joined_weight = jnp.concatenate(
        (gate_weight, up_weight, gate_adapter_first, up_adapter_first), axis=2
    )
    joined_grad = jnp.concatenate(
        (
            gate_gradient,
            upward_gradient,
            gate_part.astype(brain_float_half) * adapter_scale,
            up_part.astype(brain_float_half) * adapter_scale,
        ),
        axis=3,
    )
    input_portion = (
        jnp.einsum(
            "secf,edf->secd", joined_grad, joined_weight, preferred_element_type=single_float
        )
        .astype(brain_float_half)
        .reshape(slot_count, hidden_width)
    )
    gate_total, up_total = (
        lax.psum(gate_part.astype(jnp.bfloat16), "tensor").astype(jnp.float32),
        lax.psum(up_part.astype(jnp.bfloat16), "tensor").astype(jnp.float32),
    )
    in_slice = lax.dynamic_slice_in_dim(routed_input, slice_start, slice_width, 3)
    grad_slice = lax.dynamic_slice_in_dim(routed_gradient, slice_start, slice_width, 3)
    gate_first_gradient = adapter_scale * jnp.einsum(
        "secd,secr->edr",
        in_slice,
        gate_total.astype(brain_float_half),
        preferred_element_type=single_float,
    )
    up_first_gradient = adapter_scale * jnp.einsum(
        "secd,secr->edr",
        in_slice,
        up_total.astype(brain_float_half),
        preferred_element_type=single_float,
    )
    gate_second_gradient = adapter_scale * jnp.einsum(
        "zdbq,zdbx->dqx", adapter_gate_term, gate_gradient, preferred_element_type=single_float
    )
    up_second_gradient = adapter_scale * jnp.einsum(
        "zdbq,zdbx->dqx", adapter_up_term, upward_gradient, preferred_element_type=single_float
    )
    down_first_gradient = adapter_scale * jnp.einsum(
        "qoax,qoap->oxp",
        hidden_activation,
        backward_adapter_term,
        preferred_element_type=single_float,
    )
    down_second_gradient = adapter_scale * jnp.einsum(
        "secr,secd->erd",
        down_total.astype(brain_float_half),
        grad_slice,
        preferred_element_type=single_float,
    )
    reduced = lax.psum_scatter(
        input_portion.astype(single_float).astype(jnp.bfloat16),
        "tensor",
        scatter_dimension=1,
        tiled=True,
    ).astype(jnp.float32)
    returned = lax.all_to_all(
        reduced.astype(jnp.bfloat16), "expert", split_axis=0, concat_axis=0, tiled=True
    ).astype(reduced.dtype)
    grad_tokens = jnp.sum(returned[positions], axis=1).astype(brain_float_half)
    return (
        grad_tokens,
        gate_first_gradient,
        gate_second_gradient,
        up_first_gradient,
        up_second_gradient,
        down_first_gradient,
        down_second_gradient,
    )


def solution(mesh):
    return jax.shard_map(
        local,
        mesh=mesh,
        in_specs=(
            P("expert", "tensor"),
            P("expert", "tensor"),
            P("expert", None),
            P("expert", None),
            P("expert", None, "tensor"),
            P("expert", None, "tensor"),
            P("expert", "tensor", None),
            P("expert", None, None),
            P("expert", None, "tensor"),
            P("expert", None, None),
            P("expert", None, "tensor"),
            P("expert", "tensor", None),
            P("expert", None, None),
        ),
        out_specs=(
            P("expert", "tensor"),
            P("expert", "tensor", None),
            P("expert", None, "tensor"),
            P("expert", "tensor", None),
            P("expert", None, "tensor"),
            P("expert", "tensor", None),
            P("expert", None, "tensor"),
        ),
        check_vma=False,
    )
```

profile of v0, /device:TPU:0, one launch (start us, length us, event | category | flops | bytes accessed | tf_op | source)
XLA Modules:
  0.0 321.8 jit_solution(6364558677875069623)
XLA Ops:
  9.1 7.0 %gather_fusion.1 = f32[1024]{0:T(1024)S(1)} fusion(f32[128,16]{0,1:T(8,128)S(1)} %fusion.80, s32[1024]{0:T(1024)S(1)} %reshape.99), kind=kCustom, calls=%fused_computation.1 | custom fusion | bytes 16384 | tf_op jit(solution)/shard_map/jit(take_along_axis)/gather | solution.py:19
  16.5 5.6 %scatter_custom_fusion.1 = bf16[1536,512]{1,0:T(8,128)(2,1)S(1)} fusion(s32[1024]{0:T(1024)S(1)} %bitcast.192, bf16[]{:T(256)} %constant.14.clone.1, bf16[128,512]{1,0:T(8,128)(2,1)S(1)} %copy-done.15), kind=kCustom, calls=%fused_computation.78 | custom fusion | bytes 1703938 | tf_op jit(solution)/shard_map/scatter | solution.py:26
  22.1 44.3 %all_to_all.33 = bf16[8,192,512]{2,1,0:T(8,128)(2,1)} all-to-all(bf16[8,192,512]{2,1,0:T(8,128)(2,1)S(1)} %bitcast.190), channel_id=1, replica_groups=mesh['expert'=8,'tensor'=4] {'expert'}, dimensions={0} | all-to-all | bytes 3145728 | tf_op jit(solution)/shard_map/all_to_all | solution.py:61
  66.8 6.0 %scatter_custom_fusion = bf16[1536,512]{1,0:T(8,128)(2,1)S(1)} fusion(s32[1024]{0:T(1024)S(1)} %bitcast.193, f32[128,512]{1,0:T(8,128)S(1)} %convert_element_type.93, f32[1024]{0:T(1024)S(1)} %mul.92, bf16[]{:T(256)} %constant.14.clone.1), kind=kCustom, calls=%fused_computation.77 | custom fusion | flops 1048576 | bytes 1839106 | tf_op jit(solution)/shard_map/scatter | solution.py:26
  72.7 40.2 %all_to_all.34 = bf16[8,192,512]{2,1,0:T(8,128)(2,1)} all-to-all(bf16[8,192,512]{2,1,0:T(8,128)(2,1)S(1)} %bitcast.189), channel_id=1, replica_groups=mesh['expert'=8,'tensor'=4] {'expert'}, dimensions={0} | all-to-all | bytes 3145728 | tf_op jit(solution)/shard_map/all_to_all | solution.py:62
  116.8 3.7 %copy.81 = bf16[2,2048,192]{2,1,0:T(8,128)(2,1)} copy(bf16[2,2048,192]{1,2,0:T(8,128)(2,1)} %param.18) | data formatting | bytes 3145728 | tf_op args[5]
  120.5 2.5 copy.82
  123.0 2.5 copy.83
  125.5 5.4 %fusion.37 = bf16[8,2,96,64]{2,3,0,1:T(8,128)(2,1)S(1)} fusion(bf16[2,2048,64]{1,2,0:T(8,128)(2,1)} %param.20, bf16[8,2,96,2048]{3,2,1,0:T(8,128)(2,1)} %bitcast.194), kind=kOutput, calls=%fused_computation.61 | convolution fusion | flops 402751488 | bytes 7012352 | tf_op jit(solution)/shard_map/mbtk,bkz->mbtz/dot_general | solution.py:73
  130.9 3.1 fusion.36
  134.0 3.1 fusion.14
  137.1 3.0 fusion.16
  140.1 19.9 %all-gather.3.cloned.1.call-done = bf16[1536,2048]{1,0:T(8,128)(2,1)} async-done(((bf16[1536,512]{1,0:T(8,128)(2,1)}), bf16[1536,2048]{1,0:T(8,128)(2,1)}) %all-gather.3.cloned.1.call-update) | async-done | bytes 6291472 | tf_op jit(solution)/shard_map/all_gather | solution.py:66
  159.9 5.3 %fusion.35 = bf16[8,2,96,64]{2,3,0,1:T(8,128)(2,1)S(1)} fusion(bf16[2,64,2048]{2,1,0:T(8,128)(2,1)S(1)} %copy-done.22, bf16[8,2,96,2048]{3,2,1,0:T(8,128)(2,1)} %bitcast.200), kind=kOutput, calls=%fused_computation.59 | convolution fusion | flops 402751488 | bytes 7012352 | tf_op jit(solution)/shard_map/secd,erd->secr/dot_general | solution.py:101
  177.1 8.9 %convert_bitcast_fusion = bf16[8,2,96,2048]{3,2,0,1:T(8,128)(2,1)} fusion(bf16[2,2048,64]{2,1,0:T(8,128)(2,1)} %copy.83, bf16[2,2048,64]{2,1,0:T(8,128)(2,1)S(1)} %copy-done.6, bf16[2,2048,192]{2,1,0:T(8,128)(2,1)} %copy.81, bf16[2,2048,192]{2,1,0:T(8,128)(2,1)} %copy.80, bf16[8,2,96,64]{3,2,0,1:T(8,128)(2,1)} %copy.95, bf16[8,2,96,64]{3,2,0,1:T(8,128)(2,1)} %copy.94, ...), kind=kOutput, calls=%fused_computation.4 | convolution fusion | flops 3247439872 | bytes 12058624 | tf_op jit(solution)/shard_map/secf,edf->secd/dot_general | solution.py:136
  186.0 6.6 %copy.96 = bf16[8,2,96,2048]{3,2,1,0:T(8,128)(2,1)} copy(bf16[8,2,96,2048]{3,2,0,1:T(8,128)(2,1)} %convert_bitcast_fusion) | data formatting | bytes 12582912 | tf_op jit(solution)/shard_map/convert_element_type | solution.py:139
  192.6 58.0 %reduce-scatter.2.cloned.1.call-done = bf16[1536,512]{1,0:T(8,128)(2,1)} async-done(((bf16[1536,2048]{1,0:T(8,128)(2,1)}), bf16[1536,512]{1,0:T(8,128)(2,1)}) %reduce-scatter.2.cloned.1.call-update) | async-done | bytes 1572880 | tf_op jit(solution)/shard_map/reduce_scatter | solution.py:178
  250.6 5.6 %all-to-all-start.2 = ((bf16[8,192,512]{2,1,0:T(8,128)(2,1)}), bf16[8,192,512]{2,1,0:T(8,128)(2,1)S(1)}, u32[]{:S(2)}, u32[]{:S(2)}) async-start(bf16[8,192,512]{2,1,0:T(8,128)(2,1)} %bitcast.191), calls=%async_computation.3 | async-start | bytes 3145728 | tf_op jit(solution)/shard_map/all_to_all | solution.py:184
  262.7 32.6 %all-reduce.3.cloned.1.call-done = (bf16[8,2,96,64]{2,3,0,1:T(8,128)(2,1)}, bf16[8,2,96,64]{2,3,0,1:T(8,128)(2,1)}, bf16[8,2,96,64]{2,3,0,1:T(8,128)(2,1)}) async-done(((bf16[8,2,96,64]{2,3,0,1:T(8,128)(2,1)}, bf16[8,2,96,64]{2,3,0,1:T(8,128)(2,1)}, bf16[8,2,96,64]{2,3,0,1:T(8,128)(2,1)}), (bf16[8,2,96,64]{2,3,0,1:T(8,128)(2,1)}, bf16[8,2,96,64]{2,3,0,1:T(8,128)(2,1)}, ...) | async-done | bytes 589840 | tf_op jit(solution)/shard_map/psum | solution.py:143
  295.2 2.7 fusion.50
  297.9 2.6 fusion.56
  300.5 2.5 fusion.53
  305.2 7.3 %gather_fusion = f32[1024,512]{1,0:T(8,128)} fusion(f32[1536,512]{1,0:T(8,128)} %bitcast_convert_fusion, s32[1024]{0:T(1024)S(1)} %broadcast_clamp_fusion), kind=kCustom, calls=%fused_computation | custom fusion | bytes 4198400 | tf_op jit(solution)/shard_map/gather | solution.py:187
  312.5 2.8 bitcast_reduce_fusion
  (93 shorter events, 26.6 us)
Async XLA Ops:
  7.2 158.1 %copy-start = (bf16[2,192,2048]{2,1,0:T(8,128)(2,1)S(1)}, bf16[2,192,2048]{2,1,0:T(8,128)(2,1)}, u32[]{:S(2)}) copy-start(bf16[2,192,2048]{2,1,0:T(8,128)(2,1)} %param.19) | copy-start | bytes 4718596
  7.2 118.3 %all-gather.5.cloned.1.call-start = ((), (), s32[]{:S(2)}) async-start(), calls=%async_computation.5 | async-start | bytes 7864320 | tf_op jit(solution)/shard_map/all_gather | solution.py:65
  9.1 7.2 %copy-start.18 = (s32[128,8]{0,1:T(8,128)S(1)}, s32[128,8]{0,1:T(8,128)}, u32[]{:S(2)}) copy-start(s32[128,8]{0,1:T(8,128)} %param.16) | copy-start | bytes 12292
  9.1 7.4 %copy-start.15 = (bf16[128,512]{1,0:T(8,128)(2,1)S(1)}, bf16[128,512]{1,0:T(8,128)(2,1)}, u32[]{:S(2)}) copy-start(bf16[128,512]{1,0:T(8,128)(2,1)} %param.13) | copy-start | bytes 393220
  22.1 44.4 %copy-start.16 = (bf16[128,512]{1,0:T(8,128)(2,1)S(1)}, bf16[128,512]{1,0:T(8,128)(2,1)}, u32[]{:S(2)}) copy-start(bf16[128,512]{1,0:T(8,128)(2,1)} %param.14) | copy-start | bytes 393220
  22.1 44.5 %copy-start.19 = (f32[128,8]{0,1:T(8,128)S(1)}, f32[128,8]{0,1:T(8,128)}, u32[]{:S(2)}) copy-start(f32[128,8]{0,1:T(8,128)} %param.15) | copy-start | bytes 12292
  66.5 93.5 %all-gather.3.cloned.1.call-start = ((), (), s32[]{:S(2)}) async-start(), calls=%async_computation.4 | async-start | bytes 7864320 | tf_op jit(solution)/shard_map/all_gather | solution.py:66
  113.0 137.7 %reduce-scatter.2.cloned.1.call-start = ((), (), s32[]{:S(2)}) async-start(), calls=%async_computation.6 | async-start | bytes 7864320 | tf_op jit(solution)/shard_map/reduce_scatter | solution.py:178
  125.5 5.4 %copy-start.11 = (bf16[2,2048,64]{1,2,0:T(8,128)(2,1)S(1)}, bf16[2,2048,64]{1,2,0:T(8,128)(2,1)}, u32[]{:S(2)}) copy-start(bf16[2,2048,64]{1,2,0:T(8,128)(2,1)} %param.22) | copy-start | bytes 1572868
  125.5 5.4 %copy-start.20 = (bf16[1536,2048]{1,0:T(8,128)(2,1)S(1)}, bf16[1536,2048]{1,0:T(8,128)(2,1)}, u32[]{:S(2)}) copy-start(bf16[1536,2048]{1,0:T(8,128)(2,1)} %all-gather.5.cloned.1.call-done) | copy-start | bytes 18874372
  130.9 36.2 %copy-start.7 = (bf16[8,2,96,64]{2,3,0,1:T(8,128)(2,1)}, bf16[8,2,96,64]{2,3,0,1:T(8,128)(2,1)S(1)}, u32[]{:S(2)}) copy-start(bf16[8,2,96,64]{2,3,0,1:T(8,128)(2,1)S(1)} %fusion.37) | copy-start | bytes 589828
  134.0 3.1 copy-start.4
  137.1 22.8 %copy-start.22 = (bf16[2,64,2048]{2,1,0:T(8,128)(2,1)S(1)}, bf16[2,64,2048]{2,1,0:T(8,128)(2,1)}, u32[]{:S(2)}) copy-start(bf16[2,64,2048]{2,1,0:T(8,128)(2,1)} %param.25) | copy-start | bytes 1572868
  159.9 5.3 %copy-start.21 = (bf16[1536,2048]{1,0:T(8,128)(2,1)S(1)}, bf16[1536,2048]{1,0:T(8,128)(2,1)}, u32[]{:S(2)}) copy-start(bf16[1536,2048]{1,0:T(8,128)(2,1)} %all-gather.3.cloned.1.call-done) | copy-start | bytes 18874372
  165.3 2.3 copy-start.9
  170.9 15.2 %copy-start.2 = (bf16[8,2,96,192]{3,2,0,1:T(8,128)(2,1)}, bf16[8,2,96,192]{3,2,0,1:T(8,128)(2,1)S(1)}, u32[]{:S(2)}) copy-start(bf16[8,2,96,192]{3,2,0,1:T(8,128)(2,1)S(1)} %get-tuple-element.13) | copy-start | bytes 1769476
  170.9 6.2 %copy-start.6 = (bf16[2,2048,64]{2,1,0:T(8,128)(2,1)S(1)}, bf16[2,2048,64]{2,1,0:T(8,128)(2,1)}, u32[]{:S(2)}) copy-start(bf16[2,2048,64]{2,1,0:T(8,128)(2,1)} %copy.82) | copy-start | bytes 1572868
  250.6 7.0 %copy-start.8 = (bf16[8,2,96,64]{2,3,0,1:T(8,128)(2,1)S(1)}, bf16[8,2,96,64]{2,3,0,1:T(8,128)(2,1)}, u32[]{:S(2)}) copy-start(bf16[8,2,96,64]{2,3,0,1:T(8,128)(2,1)} %copy-done.7) | copy-start | bytes 589828
  250.6 52.4 %all-to-all-start.2 = ((bf16[8,192,512]{2,1,0:T(8,128)(2,1)}), bf16[8,192,512]{2,1,0:T(8,128)(2,1)S(1)}, u32[]{:S(2)}, u32[]{:S(2)}) async-start(bf16[8,192,512]{2,1,0:T(8,128)(2,1)} %bitcast.191), calls=%async_computation.3 | async-start | bytes 3145728 | tf_op jit(solution)/shard_map/all_to_all | solution.py:184
  256.3 39.0 %all-reduce.3.cloned.1.call-start = ((), (), s32[]{:S(2)}) async-start(), calls=%async_computation.7 | async-start | bytes 1572864 | tf_op jit(solution)/shard_map/psum | solution.py:143
  257.7 4.0 %copy-start.10 = (bf16[8,2,96,64]{2,3,0,1:T(8,128)(2,1)S(1)}, bf16[8,2,96,64]{2,3,0,1:T(8,128)(2,1)}, u32[]{:S(2)}) copy-start(bf16[8,2,96,64]{2,3,0,1:T(8,128)(2,1)} %copy-done.9) | copy-start | bytes 589828
  295.2 2.7 copy-start.24
  297.9 2.6 copy-start.23
  305.2 10.1 %copy-start.1 = (bf16[2,192,2048]{2,1,0:T(8,128)(2,1)S(1)}, bf16[2,192,2048]{2,1,0:T(8,128)(2,1)}, u32[]{:S(2)}) copy-start(bf16[2,192,2048]{2,1,0:T(8,128)(2,1)} %param.19) | copy-start | bytes 4718596
  (7 other events, 9.4 us)
Sparse Core Ops, SparseCore 0:
  66.6 45.3 all-gather.4
  113.6 46.3 all-gather.2
  192.7 57.8 reduce-scatter.1
  259.9 35.3 all-reduce.2
where the time goes:
time: 323 us; the launch traced here: 322 us
  waiting for transfers between devices  110 us (34%)
  blocking collectives  84.5 us (26%)
  matrix products  49.2 us (15%)
  local copies, waits for them, and re-layouts  45.3 us (14%)
  between operations  14.1 us (4%)
  other arithmetic  12.5 us (4%)
  starting transfers between devices  5.81 us (2%)
    reduce_scatter x1, waiting for transfers between devices, local(): lax.psum_scatter(input_portion.astype(single_float).astype(jnp.bfloat16),...  58 us
    all_to_all x1, blocking collectives, local(): lax.all_to_all(send_in, 'expert', split_axis=0, concat_axis=0, tiled=True)  44.3 us
    all_to_all x1, blocking collectives, local(): lax.all_to_all(send_grad, 'expert', split_axis=0, concat_axis=0, tiled=True)  40.2 us
    psum x1, waiting for transfers between devices, local(): lax.psum(gate_part.astype(jnp.bfloat16), 'tensor').astype(jnp.float32)  32.6 us
    all_gather x1, waiting for transfers between devices, local(): lax.all_gather(part_grad, 'tensor', axis=1, tiled=True)  19.9 us
    unnamed x57, local copies, waits for them, and re-layouts  14.2 us
    dot_general x1, matrix products, local(): jnp.einsum('secf,edf->secd', joined_grad, joined_weight, preferred_elemen...  8.95 us
    gather x5, local copies, waits for them, and re-layouts, slot_positions(): jnp.take_along_axis(before, expert_ids, axis=1).astype(jnp.int32)  7.36 us
  transfers between devices with their start and end apart: 5, of which 3 were waited for; matrix products, arithmetic and copies ran while one was open for 14% of the time, Pallas kernels for 0%

commit v1 on v0

--- a/solution.py
+++ b/solution.py
@@ -26,7 +26,7 @@
     return jnp.zeros((slot_count, width), values.dtype).at[positions.reshape(-1)].set(flat)
 
 
-def local(
+def routed_plan(
     tokens,
     grad_out,
     route_weights,
@@ -196,6 +196,184 @@
     )
 
 
+def block_diagonal(blocks):
+    count = len(blocks)
+    rows = []
+    for i, block in enumerate(blocks):
+        rows.append(
+            jnp.concatenate(
+                [block if i == j else jnp.zeros_like(blocks[j]) for j in range(count)], axis=1
+            )
+        )
+    return jnp.concatenate(rows, axis=0)
+
+
+def diagonal_blocks(matrix, count):
+    height, width = matrix.shape[0] // count, matrix.shape[1] // count
+    return jnp.stack(
+        [matrix[i * height : (i + 1) * height, i * width : (i + 1) * width] for i in range(count)]
+    )
+
+
+def widen(columns, width):
+    rows, count = columns.shape
+    return jnp.concatenate(
+        [jnp.broadcast_to(columns[:, i : i + 1], (rows, width)) for i in range(count)], axis=1
+    )
+
+
+def dot(a, b):
+    return lax.dot_general(a, b, (((1,), (0,)), ((), ())), preferred_element_type=jnp.float32)
+
+
+def dot_t(a, b):
+    return lax.dot_general(a, b, (((1,), (1,)), ((), ())), preferred_element_type=jnp.float32)
+
+
+def t_dot(a, b):
+    return lax.dot_general(a, b, (((0,), (0,)), ((), ())), preferred_element_type=jnp.float32)
+
+
+def swap_near(value):
+    count = lax.axis_size("tensor")
+    return lax.ppermute(value, "tensor", [(i, i ^ 1) for i in range(count)])
+
+
+def swap_far(value):
+    count = lax.axis_size("tensor")
+    return lax.ppermute(value, "tensor", [(i, (i + count // 2) % count) for i in range(count)])
+
+
+def pair_order(index, mine, theirs):
+    return jnp.where(index == 0, mine, theirs), jnp.where(index == 0, theirs, mine)
+
+
+def total_over_tensor(part):
+    near = part.astype(jnp.bfloat16)
+    pair = (near.astype(jnp.float32) + swap_near(near).astype(jnp.float32)).astype(jnp.bfloat16)
+    return (pair.astype(jnp.float32) + swap_far(pair).astype(jnp.float32)).astype(jnp.bfloat16)
+
+
+def dense_plan(
+    tokens,
+    grad_out,
+    route_weights,
+    expert_ids,
+    gate_weight,
+    up_weight,
+    down_weight,
+    gate_adapter_first,
+    gate_adapter_second,
+    up_adapter_first,
+    up_adapter_second,
+    down_adapter_first,
+    down_adapter_second,
+):
+    half = jnp.bfloat16
+    single = jnp.float32
+    tok_rows, width = tokens.shape
+    local_experts, hidden_width, units = gate_weight.shape
+    rank = gate_adapter_first.shape[2]
+    experts_all = local_experts * lax.axis_size("expert")
+    span = local_experts * units
+    ranks = local_experts * rank
+    place = lax.axis_index("tensor")
+    far, near = place // 2, place % 2
+
+    def half_rows(value):
+        first, second = pair_order(far, value, swap_far(value))
+        joined = jnp.concatenate((first, second), axis=1)
+        return lax.all_gather(joined, "expert", axis=0, tiled=True)
+
+    def all_features(mine):
+        even, odd = pair_order(near, mine, swap_near(mine))
+        return jnp.concatenate(
+            (even[:, :width], odd[:, :width], even[:, width:], odd[:, width:]), axis=1
+        )
+
+    tokens_half = half_rows(tokens)
+    grad_half = half_rows(grad_out)
+    numbers = lax.broadcasted_iota(jnp.int32, (1, 1, experts_all), 2)
+    chosen = jnp.sum(
+        jnp.where(expert_ids[:, :, None] == numbers, route_weights[:, :, None], 0.0), axis=1
+    )
+    chosen_all = lax.all_gather(chosen, "expert", axis=0, tiled=True)
+    factor = lax.dynamic_slice_in_dim(
+        chosen_all, lax.axis_index("expert") * local_experts, local_experts, 1
+    )
+    experts = range(local_experts)
+    joined_weight = jnp.concatenate(
+        [gate_weight[e] for e in experts]
+        + [up_weight[e] for e in experts]
+        + [gate_adapter_first[e] for e in experts]
+        + [up_adapter_first[e] for e in experts],
+        axis=1,
+    )
+    back_weight = jnp.concatenate(
+        [down_weight[e] for e in experts] + [down_adapter_second[e] for e in experts], axis=0
+    )
+    gate_second = block_diagonal([gate_adapter_second[e] for e in experts])
+    up_second = block_diagonal([up_adapter_second[e] for e in experts])
+    down_first = block_diagonal([down_adapter_first[e] for e in experts])
+    factor_units = widen(factor, units)
+    factor_ranks = widen(factor, rank)
+
+    forward = dot(all_features(tokens_half), joined_weight)
+    lora_gate = forward[:, 2 * span : 2 * span + ranks].astype(half)
+    lora_up = forward[:, 2 * span + ranks :].astype(half)
+    gate = forward[:, :span] + adapter_scale * dot(lora_gate, gate_second)
+    up = forward[:, span : 2 * span] + adapter_scale * dot(lora_up, up_second)
+    sigma = jax.nn.sigmoid(gate)
+    active = gate * sigma
+    hidden = (active * up).astype(half)
+    down_total = total_over_tensor(dot(hidden, down_first))
+
+    backward = dot_t(all_features(grad_half), back_weight)
+    back_lora = (factor_ranks * backward[:, span:]).astype(half)
+    grad_hidden = factor_units * backward[:, :span] + adapter_scale * dot_t(back_lora, down_first)
+    grad_gate = (grad_hidden * up * sigma * (1.0 + gate * (1.0 - sigma))).astype(half)
+    grad_up = (grad_hidden * active).astype(half)
+    parts = jnp.concatenate((dot_t(grad_gate, gate_second), dot_t(grad_up, up_second)), axis=1)
+    parts = parts.astype(half)
+    joined_grad = jnp.concatenate((grad_gate, grad_up, parts * adapter_scale), axis=1)
+    portion = dot_t(joined_grad, joined_weight).astype(half)
+    portion = portion.reshape(portion.shape[0], 2, 2, width)
+    keep = lax.dynamic_index_in_dim(portion, near, 2, keepdims=False)
+    give = lax.dynamic_index_in_dim(portion, 1 - near, 2, keepdims=False)
+    pair = (keep.astype(single) + swap_near(give).astype(single)).astype(half)
+    pair = pair.reshape(pair.shape[0], 2 * width)
+    summed = lax.psum_scatter(pair, "expert", scatter_dimension=0, tiled=True)
+    summed_keep = lax.dynamic_slice_in_dim(summed, far * width, width, 1)
+    summed_give = lax.dynamic_slice_in_dim(summed, (1 - far) * width, width, 1)
+    grad_tokens = (summed_keep.astype(single) + swap_far(summed_give).astype(single)).astype(half)
+
+    parts_total = total_over_tensor(parts)
+    in_slice = lax.dynamic_slice_in_dim(tokens_half, far * width, width, 1)
+    grad_slice = lax.dynamic_slice_in_dim(grad_half, far * width, width, 1)
+    first = adapter_scale * t_dot(in_slice, parts_total)
+    first = first.reshape(width, 2, local_experts, rank).transpose(1, 2, 0, 3)
+    weighted = (factor_ranks * down_total.astype(single)).astype(half)
+    down_second_gradient = adapter_scale * t_dot(weighted, grad_slice)
+    return (
+        grad_tokens,
+        first[0],
+        diagonal_blocks(adapter_scale * t_dot(lora_gate, grad_gate), local_experts),
+        first[1],
+        diagonal_blocks(adapter_scale * t_dot(lora_up, grad_up), local_experts),
+        diagonal_blocks(adapter_scale * t_dot(hidden, back_lora), local_experts),
+        down_second_gradient.reshape(local_experts, rank, width),
+    )
+
+
+def local(*arrays):
+    tok_rows, top_count = arrays[3].shape
+    local_experts = arrays[4].shape[0]
+    capacity = 3 * tok_rows * top_count // (2 * local_experts * lax.axis_size("expert"))
+    if local_experts * capacity >= tok_rows and lax.axis_size("tensor") == 2 * 2:
+        return dense_plan(*arrays)
+    return routed_plan(*arrays)
+
+
 def solution(mesh):
     return jax.shard_map(
         local,

time: 323 us -> 258 us (0.80)
  blocking collectives: 84.5 us -> 30.7 us
  matrix products: 49.2 us -> 22.6 us
  waiting for transfers between devices: 110 us -> 127 us
  other arithmetic: 12.5 us -> 8.68 us
    all_to_all x2 -> x0, blocking collectives: 84.5 us -> none  [the longest x1 44.3 us: local(): lax.all_to_all(send_in, 'expert', split_axis=0, concat_axis=0, tiled=True)]
    reduce_scatter x1 -> x0, waiting for transfers between devices: 58 us -> none  [local(): lax.psum_scatter(input_portion.astype(single_float).astype(jnp.bfloat16),...]
    unnamed x4, waiting for transfers between devices: 0.07 us -> 40.2 us
    all_gather x2, waiting for transfers between devices: 19.9 us -> 58.7 us  [half_rows(): return lax.all_gather(joined, 'expert', axis=0, tiled=True)]
    psum x1 -> x0, waiting for transfers between devices: 32.6 us -> none  [local(): lax.psum(gate_part.astype(jnp.bfloat16), 'tensor').astype(jnp.float32)]
    all_gather x0 -> x1, blocking collectives: none -> 30.7 us  [dense_plan(): chosen_all = lax.all_gather(chosen, 'expert', axis=0, tiled=True)]
    ppermute x0 -> x10, waiting for transfers between devices: none -> 28.6 us  [the longest x5 23.5 us: swap_far(): lax.ppermute(value, 'tensor', [(i, (i + count // 2) % count) for i in ran...]
    dot_general x20 -> x14, matrix products: 49.2 us -> 22.6 us  [the longest x5 9.75 us: dot_t(): lax.dot_general(a, b, (((1,), (1,)), ((), ())), preferred_element_type=jn...]
  transfers between devices with their start and end apart: 5 -> 13, of which waited for: 3 -> 10; matrix products, arithmetic and copies ran while one was open for 14% -> 9% of each run, Pallas kernels for 0% -> 0%
where the time goes in v1:
time: 258 us; the launch traced here: 257 us
  waiting for transfers between devices  127 us (49%)
  local copies, waits for them, and re-layouts  45.1 us (17%)
  blocking collectives  30.7 us (12%)
  matrix products  22.6 us (9%)
  between operations  14.2 us (6%)
  other arithmetic  8.68 us (3%)
  starting transfers between devices  8.12 us (3%)
    all_gather x2, waiting for transfers between devices, half_rows(): return lax.all_gather(joined, 'expert', axis=0, tiled=True)  58.7 us
    unnamed x4, waiting for transfers between devices  40.2 us
    all_gather x1, blocking collectives, dense_plan(): chosen_all = lax.all_gather(chosen, 'expert', axis=0, tiled=True)  30.7 us
    ppermute x5, waiting for transfers between devices, swap_far(): lax.ppermute(value, 'tensor', [(i, (i + count // 2) % count) for i in ran...  23.5 us
    unnamed x48, local copies, waits for them, and re-layouts  15.2 us
    dynamic_slice x1, local copies, waits for them, and re-layouts, dense_plan(): keep = lax.dynamic_index_in_dim(portion, near, 2, keepdims=False)  10.3 us
    dot_general x5, matrix products, dot_t(): lax.dot_general(a, b, (((1,), (1,)), ((), ())), preferred_element_type=jn...  9.75 us
    reshape x1, local copies, waits for them, and re-layouts, dense_plan(): portion = portion.reshape(portion.shape[0], 2, 2, width)  7.83 us
  transfers between devices with their start and end apart: 13, of which 10 were waited for; matrix products, arithmetic and copies ran while one was open for 9% of the time, Pallas kernels for 0%

profile of v1, /device:TPU:0, one launch (start us, length us, event | category | flops | bytes accessed | tf_op | source)
XLA Modules:
  0.0 256.8 jit_solution(708276409398479290)
XLA Ops:
  7.2 3.0 %collective-permute-start = (bf16[128,512]{1,0:T(8,128)(2,1)}, bf16[128,512]{1,0:T(8,128)(2,1)S(1)}, u32[]{:S(2)}, u32[]{:S(2)}) collective-permute-start(bf16[128,512]{1,0:T(8,128)(2,1)} %param.14), channel_id=1, source_target_pairs={{0,2},{1,3},{2,0},{3,1},{4,6},{5,7},{6,4},{7,5},{8,10},{9,11},{10,... | collective-permute-start | bytes 393224 | tf_op jit(solution)/shard_map/ppermute | solution.py:244
  10.3 4.5 %collective-permute-done = bf16[128,512]{1,0:T(8,128)(2,1)S(1)} collective-permute-done((bf16[128,512]{1,0:T(8,128)(2,1)}, bf16[128,512]{1,0:T(8,128)(2,1)S(1)}, u32[]{:S(2)}, u32[]{:S(2)}) %collective-permute-start) | collective-permute-done | bytes 131104 | tf_op jit(solution)/shard_map/ppermute | solution.py:244
  14.8 2.0 collective-permute-done.2
  27.1 42.2 %all-gather.3.cloned.1.call-done = bf16[1024,1024]{1,0:T(8,128)(2,1)} async-done(((bf16[128,1024]{1,0:T(8,128)(2,1)}), bf16[1024,1024]{1,0:T(8,128)(2,1)}) %all-gather.3.cloned.1.call-update) | async-done | bytes 2097168 | tf_op jit(solution)/shard_map/all_gather | solution.py:286
  69.3 30.7 %all_gather.9 = f32[1024,16]{0,1:T(8,128)S(1)} all-gather(f32[128,16]{0,1:T(8,128)S(1)} %select_reduce_fusion), channel_id=1, replica_groups=mesh['expert'=8,'tensor'=4] {'expert'}, dimensions={0}, use_global_device_ids=true | all-gather | bytes 73728 | tf_op jit(solution)/shard_map/all_gather | solution.py:300
  100.0 1.7 bitcast_dynamic-update-slice_fusion.5
  101.7 1.7 bitcast_dynamic-update-slice_fusion.4
  103.4 16.5 %all-gather.5.cloned.1.call-done = bf16[1024,1024]{1,0:T(8,128)(2,1)} async-done(((bf16[128,1024]{1,0:T(8,128)(2,1)}), bf16[1024,1024]{1,0:T(8,128)(2,1)}) %all-gather.5.cloned.1.call-update) | async-done | bytes 2097168 | tf_op jit(solution)/shard_map/all_gather | solution.py:286
  119.9 1.7 slice_bitcast_fusion.1
  124.9 2.0 copy-done.15
  126.9 4.5 %fusion.86 = (bf16[1024,1024]{0,1:T(8,128)(2,1)S(1)}, f32[1024,1024]{0,1:T(8,128)S(1)}) fusion(bf16[2048,1024]{0,1:T(8,128)(2,1)S(1)} %copy-done.15, bf16[1024,512]{1,0:T(8,128)(2,1)S(1)} %get-tuple-element.40, bf16[1024,512]{1,0:T(8,128)(2,1)S(1)} %get-tuple-element.38, bf16[1024,512]{1,0:T(8,128)(2,1)S(1)} %get-tuple-element.39, ...), kind=kOutput, calls=%fused_computation.156 | convolution fusion | flops 4312793088 | bytes 14680064 | tf_op jit(solution)/shard_map/dot_general | solution.py:226
  131.9 2.4 fusion
  135.5 2.0 multiply_convert_fusion
  139.1 6.3 %convolution_convert_fusion = bf16[1024,2048]{1,0:T(8,128)(2,1)} fusion(bf16[2048,1024]{0,1:T(8,128)(2,1)S(1)} %copy-done.15, bf16[1024,256]{0,1:T(8,128)(2,1)S(1)} %get-tuple-element.50, bf16[1024,384]{0,1:T(8,128)(2,1)S(1)} %get-tuple-element.36, bf16[1024,384]{0,1:T(8,128)(2,1)S(1)} %get-tuple-element.35), kind=kOutput, calls=%fused_computation.18 | convolution fusion | flops 4303355904 | bytes 10485760 | tf_op jit(solution)/shard_map/dot_general | solution.py:230
  145.4 7.8 %reshape.30 = bf16[1024,2,2,512]{3,2,1,0:T(2,128)(2,1)} reshape(bf16[1024,2048]{1,0:T(8,128)(2,1)} %convolution_convert_fusion) | data formatting | bytes 8388608 | tf_op jit(solution)/shard_map/reshape | solution.py:340
  153.2 10.3 %constant_dynamic-slice_fusion.4 = (bf16[1024,2,1,512]{3,2,1,0:T(2,128)(2,1)S(1)}, bf16[1024,2,1,512]{3,2,1,0:T(2,128)(2,1)S(1)}) fusion(bf16[1024,2,2,512]{3,2,1,0:T(2,128)(2,1)} %reshape.30, s32[]{:T(128)S(6)} %select_n.87, s32[]{:T(128)S(6)} %select_n.88), kind=kLoop, calls=%fused_computation.130 | loop fusion | bytes 8388616 | tf_op jit(solution)/shard_map/jit(dynamic_index_in_dim)/dynamic_slice | solution.py:341
  164.8 3.8 %collective-permute-done.4 = bf16[1024,2,512]{2,0,1:T(8,128)(2,1)S(1)} collective-permute-done((bf16[1024,2,512]{2,0,1:T(8,128)(2,1)S(1)}, bf16[1024,2,512]{2,0,1:T(8,128)(2,1)S(1)}, u32[]{:S(2)}, u32[]{:S(2)}) %collective-permute-start.4) | collective-permute-done | bytes 2097184 | tf_op jit(solution)/shard_map/ppermute | solution.py:239
  168.6 2.2 fusion.16
  170.8 3.0 %copy.44 = bf16[1024,2,512]{0,2,1:T(8,128)(2,1)S(1)} copy(bf16[1024,2,512]{2,0,1:T(8,128)(2,1)} %fusion.16) | data formatting | bytes 4194304 | tf_op jit(solution)/shard_map/convert_element_type | solution.py:343
  173.8 2.6 %copy.48 = bf16[1024,1024]{1,0:T(8,128)(2,1)} copy(bf16[1024,1024]{0,1:T(8,128)(2,1)S(1)} %bitcast.76) | data formatting | bytes 4194304
  187.2 4.9 %collective-permute-done.9 = bf16[1024,128]{0,1:T(8,128)(2,1)S(1)} collective-permute-done((bf16[1024,128]{0,1:T(8,128)(2,1)S(1)}, bf16[1024,128]{0,1:T(8,128)(2,1)S(1)}, u32[]{:S(2)}, u32[]{:S(2)}) %collective-permute-start.9) | collective-permute-done | bytes 262176 | tf_op jit(solution)/shard_map/ppermute | solution.py:244
  193.1 9.6 %collective-permute-done.7 = bf16[1024,256]{0,1:T(8,128)(2,1)S(1)} collective-permute-done((bf16[1024,256]{0,1:T(8,128)(2,1)S(1)}, bf16[1024,256]{0,1:T(8,128)(2,1)S(1)}, u32[]{:S(2)}, u32[]{:S(2)}) %collective-permute-start.7) | collective-permute-done | bytes 524320 | tf_op jit(solution)/shard_map/ppermute | solution.py:244
  203.2 40.1 %reduce-scatter.4.cloned.1.call-done = bf16[128,1024]{1,0:T(8,128)(2,1)} async-done(((bf16[1024,1024]{1,0:T(8,128)(2,1)}), bf16[128,1024]{1,0:T(8,128)(2,1)}) %reduce-scatter.4.cloned.1.call-update) | async-done | bytes 262160
  247.0 2.5 collective-permute-done.5
  (105 shorter events, 34.7 us)
Async XLA Ops:
  7.2 13.1 %copy-start.4 = (bf16[2,2048,192]{1,2,0:T(8,128)(2,1)S(1)}, bf16[2,2048,192]{1,2,0:T(8,128)(2,1)}, u32[]{:S(2)}) copy-start(bf16[2,2048,192]{1,2,0:T(8,128)(2,1)} %param.17) | copy-start | bytes 4718596
  7.2 62.1 %all-gather.3.cloned.1.call-start = ((), (), s32[]{:S(2)}) async-start(), calls=%async_computation.1 | async-start | bytes 2359296 | tf_op jit(solution)/shard_map/all_gather | solution.py:286
  7.2 7.6 %collective-permute-start = (bf16[128,512]{1,0:T(8,128)(2,1)}, bf16[128,512]{1,0:T(8,128)(2,1)S(1)}, u32[]{:S(2)}, u32[]{:S(2)}) collective-permute-start(bf16[128,512]{1,0:T(8,128)(2,1)} %param.14), channel_id=1, source_target_pairs={{0,2},{1,3},{2,0},{3,1},{4,6},{5,7},{6,4},{7,5},{8,10},{9,11},{10,... | collective-permute-start | bytes 393224 | tf_op jit(solution)/shard_map/ppermute | solution.py:244
  10.3 6.5 %collective-permute-start.2 = (bf16[128,512]{1,0:T(8,128)(2,1)}, bf16[128,512]{1,0:T(8,128)(2,1)S(1)}, u32[]{:S(2)}, u32[]{:S(2)}) collective-permute-start(bf16[128,512]{1,0:T(8,128)(2,1)} %param.13), channel_id=1, source_target_pairs={{0,2},{1,3},{2,0},{3,1},{4,6},{5,7},{6,4},{7,5},{8,10},{9,11},{10,... | collective-permute-start | bytes 393224 | tf_op jit(solution)/shard_map/ppermute | solution.py:244
  18.5 101.3 %all-gather.5.cloned.1.call-start = ((), (), s32[]{:S(2)}) async-start(), calls=%async_computation.2 | async-start | bytes 2359296 | tf_op jit(solution)/shard_map/all_gather | solution.py:286
  19.4 4.4 %copy-start.5 = (bf16[2,2048,192]{1,2,0:T(8,128)(2,1)S(1)}, bf16[2,2048,192]{1,2,0:T(8,128)(2,1)}, u32[]{:S(2)}) copy-start(bf16[2,2048,192]{1,2,0:T(8,128)(2,1)} %param.18) | copy-start | bytes 4718596
  22.0 221.3 %reduce-scatter.4.cloned.1.call-start = ((), (), s32[]{:S(2)}) async-start(), calls=%async_computation.3 | async-start | bytes 2359296
  22.8 2.8 %copy-start.11 = (bf16[2,2048,64]{1,2,0:T(8,128)(2,1)S(1)}, bf16[2,2048,64]{1,2,0:T(8,128)(2,1)}, u32[]{:S(2)}) copy-start(bf16[2,2048,64]{1,2,0:T(8,128)(2,1)} %param.20) | copy-start | bytes 1572868
  23.8 45.5 %copy-start.16 = (f32[128,8]{0,1:T(8,128)S(1)}, f32[128,8]{0,1:T(8,128)}, u32[]{:S(2)}) copy-start(f32[128,8]{0,1:T(8,128)} %param.15) | copy-start | bytes 12292
  23.8 45.5 %copy-start.17 = (s32[128,8]{0,1:T(8,128)S(1)}, s32[128,8]{0,1:T(8,128)}, u32[]{:S(2)}) copy-start(s32[128,8]{0,1:T(8,128)} %param.16) | copy-start | bytes 12292
  25.7 94.2 %copy-start.12 = (bf16[2,64,2048]{2,1,0:T(8,128)(2,1)S(1)}, bf16[2,64,2048]{2,1,0:T(8,128)(2,1)}, u32[]{:S(2)}) copy-start(bf16[2,64,2048]{2,1,0:T(8,128)(2,1)} %param.25) | copy-start | bytes 1572868
  69.3 52.3 %collective-permute-start.1 = (bf16[1024,1024]{1,0:T(8,128)(2,1)}, bf16[1024,1024]{1,0:T(8,128)(2,1)S(1)}, u32[]{:S(2)}, u32[]{:S(2)}) collective-permute-start(bf16[1024,1024]{1,0:T(8,128)(2,1)} %all-gather.3.cloned.1.call-done), channel_id=1, source_target_pairs={{0,1},{1,0},{2,3},{3,2},{4,5},{5,4},{6,7},{7,6},{8,9},{9,8},{10,11... | collective-permute-start | bytes 6291464 | tf_op jit(solution)/shard_map/ppermute | solution.py:239
  119.8 4.4 %collective-permute-start.3 = (bf16[1024,1024]{1,0:T(8,128)(2,1)}, bf16[1024,1024]{1,0:T(8,128)(2,1)S(1)}, u32[]{:S(2)}, u32[]{:S(2)}) collective-permute-start(bf16[1024,1024]{1,0:T(8,128)(2,1)} %all-gather.5.cloned.1.call-done), channel_id=1, source_target_pairs={{0,1},{1,0},{2,3},{3,2},{4,5},{5,4},{6,7},{7,6},{8,9},{9,8},{10,11... | collective-permute-start | bytes 6291464 | tf_op jit(solution)/shard_map/ppermute | solution.py:239
  131.4 4.1 %copy-start.14 = (bf16[1024,1024]{0,1:T(8,128)(2,1)}, bf16[1024,1024]{0,1:T(8,128)(2,1)S(1)}, u32[]{:S(2)}) copy-start(bf16[1024,1024]{0,1:T(8,128)(2,1)S(1)} %get-tuple-element.73) | copy-start | bytes 6291460
  164.2 4.4 %collective-permute-start.4 = (bf16[1024,2,512]{2,0,1:T(8,128)(2,1)S(1)}, bf16[1024,2,512]{2,0,1:T(8,128)(2,1)S(1)}, u32[]{:S(2)}, u32[]{:S(2)}) collective-permute-start(bf16[1024,2,512]{2,0,1:T(8,128)(2,1)S(1)} %bitcast.77), channel_id=1, source_target_pairs={{0,1},{1,0},{2,3},{3,2},{4,5},{5,4},{6,7},{7,6},{8,9},{9,8},{10,11... | collective-permute-start | bytes 6291464 | tf_op jit(solution)/shard_map/ppermute | solution.py:239
  176.4 3.5 %copy-start.9 = (bf16[1024,384]{0,1:T(8,128)(2,1)S(1)}, bf16[1024,384]{0,1:T(8,128)(2,1)}, u32[]{:S(2)}) copy-start(bf16[1024,384]{0,1:T(8,128)(2,1)} %copy-done.8) | copy-start | bytes 2359300
  177.5 3.7 %copy-start.7 = (bf16[1024,384]{0,1:T(8,128)(2,1)S(1)}, bf16[1024,384]{0,1:T(8,128)(2,1)}, u32[]{:S(2)}) copy-start(bf16[1024,384]{0,1:T(8,128)(2,1)} %copy-done.6) | copy-start | bytes 2359300
  177.8 4.9 %collective-permute-start.8 = (bf16[1024,128]{0,1:T(8,128)(2,1)S(1)}, bf16[1024,128]{0,1:T(8,128)(2,1)S(1)}, u32[]{:S(2)}, u32[]{:S(2)}) collective-permute-start(bf16[1024,128]{0,1:T(8,128)(2,1)S(1)} %convolution_convert_fusion.1), channel_id=1, source_target_pairs={{0,1},{1,0},{2,3},{3,2},{4,5},{5,4},{6,7},{7,6},{8,9},{9,8},{10,11... | collective-permute-start | bytes 786440 | tf_op jit(solution)/shard_map/ppermute | solution.py:239
  178.2 6.1 %collective-permute-start.6 = (bf16[1024,256]{0,1:T(8,128)(2,1)}, bf16[1024,256]{0,1:T(8,128)(2,1)S(1)}, u32[]{:S(2)}, u32[]{:S(2)}) collective-permute-start(bf16[1024,256]{0,1:T(8,128)(2,1)} %get-tuple-element.49), channel_id=1, source_target_pairs={{0,1},{1,0},{2,3},{3,2},{4,5},{5,4},{6,7},{7,6},{8,9},{9,8},{10,11... | collective-permute-start | bytes 1572872 | tf_op jit(solution)/shard_map/ppermute | solution.py:239
  182.6 9.5 %copy-start.1 = (bf16[1024,1024]{1,0:T(8,128)(2,1)S(1)}, bf16[1024,1024]{1,0:T(8,128)(2,1)}, u32[]{:S(2)}) copy-start(bf16[1024,1024]{1,0:T(8,128)(2,1)} %all-gather.3.cloned.1.call-done) | copy-start | bytes 6291460
  182.8 19.9 %copy-start.3 = (bf16[1024,1024]{1,0:T(8,128)(2,1)S(1)}, bf16[1024,1024]{1,0:T(8,128)(2,1)}, u32[]{:S(2)}) copy-start(bf16[1024,1024]{1,0:T(8,128)(2,1)} %all-gather.5.cloned.1.call-done) | copy-start | bytes 6291460
  182.8 9.2 %collective-permute-start.9 = (bf16[1024,128]{0,1:T(8,128)(2,1)S(1)}, bf16[1024,128]{0,1:T(8,128)(2,1)S(1)}, u32[]{:S(2)}, u32[]{:S(2)}) collective-permute-start(bf16[1024,128]{0,1:T(8,128)(2,1)S(1)} %add_convert_fusion.4), channel_id=1, source_target_pairs={{0,2},{1,3},{2,0},{3,1},{4,6},{5,7},{6,4},{7,5},{8,10},{9,11},{10,... | collective-permute-start | bytes 786440 | tf_op jit(solution)/shard_map/ppermute | solution.py:244
  184.5 18.2 %collective-permute-start.7 = (bf16[1024,256]{0,1:T(8,128)(2,1)S(1)}, bf16[1024,256]{0,1:T(8,128)(2,1)S(1)}, u32[]{:S(2)}, u32[]{:S(2)}) collective-permute-start(bf16[1024,256]{0,1:T(8,128)(2,1)S(1)} %add_convert_fusion.1), channel_id=1, source_target_pairs={{0,2},{1,3},{2,0},{3,1},{4,6},{5,7},{6,4},{7,5},{8,10},{9,11},{10,... | collective-permute-start | bytes 1572872 | tf_op jit(solution)/shard_map/ppermute | solution.py:244
  244.4 5.0 %collective-permute-start.5 = (bf16[128,512]{0,1:T(8,128)(2,1)S(1)}, bf16[128,512]{0,1:T(8,128)(2,1)S(1)}, u32[]{:S(2)}, u32[]{:S(2)}) collective-permute-start(bf16[128,512]{0,1:T(8,128)(2,1)S(1)} %copy.53), channel_id=1, source_target_pairs={{0,2},{1,3},{2,0},{3,1},{4,6},{5,7},{6,4},{7,5},{8,10},{9,11},{10,... | collective-permute-start | bytes 393224 | tf_op jit(solution)/shard_map/ppermute | solution.py:244
  (7 other events, 11.4 us)
Sparse Core Ops, SparseCore 0:
  18.7 50.5 all-gather.2
  72.0 47.8 all-gather.4
  176.5 66.7 reduce-scatter.3

commit v2 on v1

--- a/solution.py
+++ b/solution.py
@@ -1,6 +1,10 @@
+import functools
+
 import jax
 import jax.numpy as jnp
 from jax import lax
+from jax.experimental import pallas as pl
+from jax.experimental.pallas import tpu as pltpu
 from jax.sharding import PartitionSpec as P
 
 adapter_scale = 0.5
@@ -244,14 +248,200 @@
     return lax.ppermute(value, "tensor", [(i, (i + count // 2) % count) for i in range(count)])
 
 
-def pair_order(index, mine, theirs):
-    return jnp.where(index == 0, mine, theirs), jnp.where(index == 0, theirs, mine)
-
-
 def total_over_tensor(part):
     near = part.astype(jnp.bfloat16)
     pair = (near.astype(jnp.float32) + swap_near(near).astype(jnp.float32)).astype(jnp.bfloat16)
     return (pair.astype(jnp.float32) + swap_far(pair).astype(jnp.float32)).astype(jnp.bfloat16)
+
+
+def gather_kernel(
+    count,
+    tokens_ref,
+    grad_ref,
+    chosen_ref,
+    mine_ref,
+    theirs_ref,
+    chosen_all_ref,
+    local_sem,
+    far_send,
+    far_recv,
+    ring_send,
+    ring_recv,
+    near_send,
+    near_recv,
+    small_send,
+    small_recv,
+):
+    me = lax.axis_index("expert")
+    place = lax.axis_index("tensor")
+    far, near = place // 2, place % 2
+    rows, width = tokens_ref.shape
+    depth = count // 2
+    side = me % 2
+    position = (1 - side) * (me // 2) + side * (count - 1 - me // 2)
+
+    def expert_at(ring_place):
+        ring_place = (ring_place + 2 * count) % count
+        second = ring_place // depth
+        return (1 - second) * 2 * ring_place + second * (2 * (count - 1 - ring_place) + 1)
+
+    far_device = {"tensor": (1 - far) * 2 + near}
+    near_device = {"tensor": far * 2 + 1 - near}
+    barrier = pltpu.get_barrier_semaphore()
+    pl.semaphore_signal(
+        barrier, inc=1, device_id=far_device, device_id_type=pl.DeviceIdType.MESH
+    )
+    pl.semaphore_signal(
+        barrier, inc=1, device_id=near_device, device_id_type=pl.DeviceIdType.MESH
+    )
+    for i in range(1, count):
+        pl.semaphore_signal(
+            barrier,
+            inc=1,
+            device_id={"expert": (me + i) % count},
+            device_id_type=pl.DeviceIdType.MESH,
+        )
+    pl.semaphore_wait(barrier, count + 1)
+
+    def remote(src, dst, send, recv, device):
+        return pltpu.make_async_remote_copy(
+            src_ref=src,
+            dst_ref=dst,
+            send_sem=send,
+            recv_sem=recv,
+            device_id=device,
+            device_id_type=pl.DeviceIdType.MESH,
+        )
+
+    def columns(array, owner):
+        return pl.ds(pl.multiple_of((2 * array + owner) * width, 128), width)
+
+    sends, arrivals = [], []
+    sources = (tokens_ref, grad_ref)
+    for i, source in enumerate(sources):
+        copy = remote(
+            source,
+            mine_ref.at[me, :, columns(i, far)],
+            far_send.at[i],
+            far_recv.at[i],
+            far_device,
+        )
+        copy.start()
+        sends.append(copy)
+    own = [
+        pltpu.make_async_copy(source, mine_ref.at[me, :, columns(i, far)], local_sem.at[i])
+        for i, source in enumerate(sources)
+    ]
+    own.append(pltpu.make_async_copy(chosen_ref, chosen_all_ref.at[me], local_sem.at[2]))
+    for copy in own:
+        copy.start()
+    for i in range(1, count):
+        copy = remote(
+            chosen_ref,
+            chosen_all_ref.at[me],
+            small_send.at[i - 1],
+            small_recv.at[i - 1],
+            {"expert": (me + i) % count},
+        )
+        copy.start()
+        sends.append(copy)
+        arrivals.append(
+            remote(
+                chosen_ref,
+                chosen_all_ref.at[(me + count - i) % count],
+                small_send.at[i - 1],
+                small_recv.at[i - 1],
+                {"expert": (me + i) % count},
+            )
+        )
+    for copy in own:
+        copy.wait()
+    for i, source in enumerate(sources):
+        remote(
+            source,
+            mine_ref.at[me, :, columns(i, 1 - far)],
+            far_send.at[i],
+            far_recv.at[i],
+            far_device,
+        ).wait_recv()
+
+    def share(block, slot):
+        copy = remote(
+            mine_ref.at[block],
+            theirs_ref.at[block],
+            near_send.at[slot],
+            near_recv.at[slot],
+            near_device,
+        )
+        copy.start()
+        sends.append(copy)
+        arrivals.append(copy)
+
+    def part(step, way, block):
+        if step < depth - 1:
+            return mine_ref.at[block]
+        return mine_ref.at[block, pl.ds(way * (rows // 2), rows // 2)]
+
+    for step in range(depth):
+        for way, sign in ((0, 1), (1, -1)):
+            block = expert_at(position - sign * step)
+            piece = part(step, way, block)
+            copy = remote(
+                piece,
+                piece,
+                ring_send.at[way, step],
+                ring_recv.at[way, step],
+                {"expert": expert_at(position + sign)},
+            )
+            copy.start()
+            sends.append(copy)
+        if step == 0:
+            share(me, 0)
+        else:
+            for way, sign in ((0, 1), (1, -1)):
+                share(expert_at(position - sign * step), 2 * step - 1 + way)
+        for way, sign in ((0, 1), (1, -1)):
+            block = expert_at(position - sign * (step + 1))
+            piece = part(step, way, block)
+            remote(
+                piece,
+                piece,
+                ring_send.at[way, step],
+                ring_recv.at[way, step],
+                {"expert": expert_at(position + sign)},
+            ).wait_recv()
+    share(expert_at(position + depth), count - 1)
+    for copy in arrivals:
+        copy.wait_recv()
+    for copy in sends:
+        copy.wait_send()
+
+
+def gather_all(tokens, grad_out, chosen):
+    count = lax.axis_size("expert")
+    rows, width = tokens.shape
+    block = jax.ShapeDtypeStruct((count, rows, 4 * width), tokens.dtype)
+    dma = pltpu.SemaphoreType.DMA
+    return pl.pallas_call(
+        functools.partial(gather_kernel, count),
+        out_shape=(block, block, jax.ShapeDtypeStruct((count,) + chosen.shape, chosen.dtype)),
+        in_specs=[pl.BlockSpec(memory_space=pltpu.VMEM)] * 3,
+        out_specs=[pl.BlockSpec(memory_space=pltpu.VMEM)] * 3,
+        scratch_shapes=[
+            dma((3,)),
+            dma((2,)),
+            dma((2,)),
+            dma((2, count // 2)),
+            dma((2, count // 2)),
+            dma((count,)),
+            dma((count,)),
+            dma((count - 1,)),
+            dma((count - 1,)),
+        ],
+        compiler_params=pltpu.CompilerParams(
+            collective_id=0, has_side_effects=True, vmem_limit_bytes=32 * 2**20
+        ),
+    )(tokens, grad_out, chosen)
 
 
 def dense_plan(
@@ -280,45 +470,42 @@
     place = lax.axis_index("tensor")
     far, near = place // 2, place % 2
 
-    def half_rows(value):
-        first, second = pair_order(far, value, swap_far(value))
-        joined = jnp.concatenate((first, second), axis=1)
-        return lax.all_gather(joined, "expert", axis=0, tiled=True)
-
-    def all_features(mine):
-        even, odd = pair_order(near, mine, swap_near(mine))
-        return jnp.concatenate(
-            (even[:, :width], odd[:, :width], even[:, width:], odd[:, width:]), axis=1
-        )
-
-    tokens_half = half_rows(tokens)
-    grad_half = half_rows(grad_out)
     numbers = lax.broadcasted_iota(jnp.int32, (1, 1, experts_all), 2)
     chosen = jnp.sum(
         jnp.where(expert_ids[:, :, None] == numbers, route_weights[:, :, None], 0.0), axis=1
     )
-    chosen_all = lax.all_gather(chosen, "expert", axis=0, tiled=True)
-    factor = lax.dynamic_slice_in_dim(
+    mine, theirs, chosen_all = gather_all(tokens, grad_out, chosen.T)
+    mine = mine.reshape(-1, 4 * width)
+    theirs = theirs.reshape(-1, 4 * width)
+    chosen_all = lax.dynamic_slice_in_dim(
         chosen_all, lax.axis_index("expert") * local_experts, local_experts, 1
     )
+    factor = chosen_all.transpose(0, 2, 1).reshape(-1, local_experts)
     experts = range(local_experts)
-    joined_weight = jnp.concatenate(
-        [gate_weight[e] for e in experts]
-        + [up_weight[e] for e in experts]
-        + [gate_adapter_first[e] for e in experts]
-        + [up_adapter_first[e] for e in experts],
-        axis=1,
-    )
-    back_weight = jnp.concatenate(
-        [down_weight[e] for e in experts] + [down_adapter_second[e] for e in experts], axis=0
-    )
+
+    def pick(weight, core, axis):
+        pieces = [
+            lax.dynamic_slice_in_dim(weight, (2 * i + core) * width, width, axis) for i in range(2)
+        ]
+        return jnp.concatenate(pieces, axis=axis)
+
+    def joined_rows(core):
+        arrays = (gate_weight, up_weight, gate_adapter_first, up_adapter_first)
+        return jnp.concatenate([pick(w[e], core, 0) for w in arrays for e in experts], axis=1)
+
+    def back_columns(core):
+        arrays = (down_weight, down_adapter_second)
+        return jnp.concatenate([pick(w[e], core, 1) for w in arrays for e in experts], axis=0)
+
+    joined_keep, joined_give = joined_rows(near), joined_rows(1 - near)
+    back_keep, back_give = back_columns(near), back_columns(1 - near)
     gate_second = block_diagonal([gate_adapter_second[e] for e in experts])
     up_second = block_diagonal([up_adapter_second[e] for e in experts])
     down_first = block_diagonal([down_adapter_first[e] for e in experts])
     factor_units = widen(factor, units)
     factor_ranks = widen(factor, rank)
 
-    forward = dot(all_features(tokens_half), joined_weight)
+    forward = dot(mine[:, : 2 * width], joined_keep) + dot(theirs[:, : 2 * width], joined_give)
     lora_gate = forward[:, 2 * span : 2 * span + ranks].astype(half)
     lora_up = forward[:, 2 * span + ranks :].astype(half)
     gate = forward[:, :span] + adapter_scale * dot(lora_gate, gate_second)
@@ -328,7 +515,7 @@
     hidden = (active * up).astype(half)
     down_total = total_over_tensor(dot(hidden, down_first))
 
-    backward = dot_t(all_features(grad_half), back_weight)
+    backward = dot_t(mine[:, 2 * width :], back_keep) + dot_t(theirs[:, 2 * width :], back_give)
     back_lora = (factor_ranks * backward[:, span:]).astype(half)
     grad_hidden = factor_units * backward[:, :span] + adapter_scale * dot_t(back_lora, down_first)
     grad_gate = (grad_hidden * up * sigma * (1.0 + gate * (1.0 - sigma))).astype(half)
@@ -336,20 +523,17 @@
     parts = jnp.concatenate((dot_t(grad_gate, gate_second), dot_t(grad_up, up_second)), axis=1)
     parts = parts.astype(half)
     joined_grad = jnp.concatenate((grad_gate, grad_up, parts * adapter_scale), axis=1)
-    portion = dot_t(joined_grad, joined_weight).astype(half)
-    portion = portion.reshape(portion.shape[0], 2, 2, width)
-    keep = lax.dynamic_index_in_dim(portion, near, 2, keepdims=False)
-    give = lax.dynamic_index_in_dim(portion, 1 - near, 2, keepdims=False)
-    pair = (keep.astype(single) + swap_near(give).astype(single)).astype(half)
-    pair = pair.reshape(pair.shape[0], 2 * width)
+    give = swap_near(dot_t(joined_grad, joined_give).astype(half))
+    keep = dot_t(joined_grad, joined_keep).astype(half)
+    pair = (keep.astype(single) + give.astype(single)).astype(half)
     summed = lax.psum_scatter(pair, "expert", scatter_dimension=0, tiled=True)
     summed_keep = lax.dynamic_slice_in_dim(summed, far * width, width, 1)
     summed_give = lax.dynamic_slice_in_dim(summed, (1 - far) * width, width, 1)
     grad_tokens = (summed_keep.astype(single) + swap_far(summed_give).astype(single)).astype(half)
 
     parts_total = total_over_tensor(parts)
-    in_slice = lax.dynamic_slice_in_dim(tokens_half, far * width, width, 1)
-    grad_slice = lax.dynamic_slice_in_dim(grad_half, far * width, width, 1)
+    in_slice = lax.dynamic_slice_in_dim(mine, far * width, width, 1)
+    grad_slice = lax.dynamic_slice_in_dim(mine, (2 + far) * width, width, 1)
     first = adapter_scale * t_dot(in_slice, parts_total)
     first = first.reshape(width, 2, local_experts, rank).transpose(1, 2, 0, 3)
     weighted = (factor_ranks * down_total.astype(single)).astype(half)

time: 258 us -> 189 us (0.73)
  waiting for transfers between devices: 127 us -> 60.4 us
  Pallas kernels: 0 us -> 56 us
  blocking collectives: 30.7 us -> 0 us
  local copies, waits for them, and re-layouts: 45.1 us -> 23 us
  other arithmetic: 8.68 us -> 5.15 us
  starting transfers between devices: 8.12 us -> 4.74 us
    all_gather x2 -> x0, waiting for transfers between devices: 58.7 us -> none  [half_rows(): return lax.all_gather(joined, 'expert', axis=0, tiled=True)]
    pallas_call x0 -> x1, Pallas kernels: none -> 56 us  [gather_all(): pl.pallas_call(functools.partial(gather_kernel, count), out_shape=(block,...]
    reduce_scatter x0 -> x1, waiting for transfers between devices: none -> 40.6 us  [dense_plan(): summed = lax.psum_scatter(pair, 'expert', scatter_dimension=0, tiled=True)]
    unnamed x4 -> x1, waiting for transfers between devices: 40.2 us -> 0.02 us
    all_gather x1 -> x0, blocking collectives: 30.7 us -> none  [dense_plan(): chosen_all = lax.all_gather(chosen, 'expert', axis=0, tiled=True)]
    reshape x1, local copies, waits for them, and re-layouts: 7.83 us -> 0.01 us  [dense_plan(): factor = chosen_all.transpose(0, 2, 1).reshape(-1, local_experts)]
    ppermute x5 -> x3, waiting for transfers between devices: 23.5 us -> 16 us  [swap_far(): lax.ppermute(value, 'tensor', [(i, (i + count // 2) % count) for i in ran...]
    dynamic_slice x2 -> x7, local copies, waits for them, and re-layouts: 11.3 us -> 3.89 us  [the longest x6 2.97 us: pick(): lax.dynamic_slice_in_dim(weight, (2 * i + core) * width, width, axis)]
  transfers between devices with their start and end apart: 13 -> 7, of which waited for: 10 -> 5; matrix products, arithmetic and copies ran while one was open for 9% -> 6% of each run, Pallas kernels for 0% -> 0%
where the time goes in v2:
time: 189 us; the launch traced here: 188 us
  waiting for transfers between devices  60.4 us (32%)
  Pallas kernels  56 us (30%)
  matrix products  24.6 us (13%)
  local copies, waits for them, and re-layouts  23 us (12%)
  between operations  14.6 us (8%)
  other arithmetic  5.15 us (3%)
  starting transfers between devices  4.74 us (3%)
    pallas_call x1, Pallas kernels, gather_all(): pl.pallas_call(functools.partial(gather_kernel, count), out_shape=(block,...  56 us
    reduce_scatter x1, waiting for transfers between devices, dense_plan(): summed = lax.psum_scatter(pair, 'expert', scatter_dimension=0, tiled=True)  40.6 us
    ppermute x3, waiting for transfers between devices, swap_far(): lax.ppermute(value, 'tensor', [(i, (i + count // 2) % count) for i in ran...  16 us
    dot_general x7, matrix products, dot_t(): lax.dot_general(a, b, (((1,), (1,)), ((), ())), preferred_element_type=jn...  10 us
    unnamed x40, local copies, waits for them, and re-layouts  8.7 us
    dot_general x5, matrix products, t_dot(): lax.dot_general(a, b, (((0,), (0,)), ((), ())), preferred_element_type=jn...  7.97 us
    dot_general x5, matrix products, dot(): lax.dot_general(a, b, (((1,), (0,)), ((), ())), preferred_element_type=jn...  6.57 us
    slice x4, local copies, waits for them, and re-layouts, joined_rows(): w[e]  5.11 us
  transfers between devices with their start and end apart: 7, of which 5 were waited for; matrix products, arithmetic and copies ran while one was open for 6% of the time, Pallas kernels for 0%

profile of v2, /device:TPU:0, one launch (start us, length us, event | category | flops | bytes accessed | tf_op | source)
XLA Modules:
  0.0 188.4 jit_solution(2837127418601721397)
XLA Ops:
  8.2 1.4 slice_bitcast_fusion.11
  10.4 1.9 fusion.104
  12.2 1.9 fusion.103
  18.6 56.0 %shard_map.180 = (bf16[8,128,2048]{2,1,0:T(8,128)(2,1)S(1)}, bf16[8,128,2048]{2,1,0:T(8,128)(2,1)S(1)}, f32[8,16,128]{2,1,0:T(8,128)S(1)}) custom-call(bf16[128,512]{1,0:T(8,128)(2,1)S(1)} %copy-done.2, bf16[128,512]{1,0:T(8,128)(2,1)S(1)} %copy-done.3, f32[16,128]{1,0:T(8,128)S(1)} %bitcast.151), custom_call_target="tpu_custom_call" | custom-call | tf_op jit(solution)/shard_map/pallas_call | solution.py:425
  74.6 2.0 %copy-done = bf16[8,128,2048]{2,1,0:T(8,128)(2,1)} copy-done((bf16[8,128,2048]{2,1,0:T(8,128)(2,1)}, bf16[8,128,2048]{2,1,0:T(8,128)(2,1)S(1)}, u32[]{:S(2)}) %copy-start) | copy-done | bytes 4194328
  76.6 2.0 %copy-done.4 = bf16[8,128,2048]{2,1,0:T(8,128)(2,1)} copy-done((bf16[8,128,2048]{2,1,0:T(8,128)(2,1)}, bf16[8,128,2048]{2,1,0:T(8,128)(2,1)S(1)}, u32[]{:S(2)}) %copy-start.4) | copy-done | bytes 4194328
  82.0 1.9 %copy-done.5 = bf16[8,128,2048]{2,1,0:T(8,128)(2,1)S(1)} copy-done((bf16[8,128,2048]{2,1,0:T(8,128)(2,1)S(1)}, bf16[8,128,2048]{2,1,0:T(8,128)(2,1)}, u32[]{:S(2)}) %copy-start.5) | copy-done | bytes 4194328
  84.0 2.4 %fusion = f32[1024,1024]{0,1:T(8,128)S(1)} fusion(bf16[1024,1024]{0,1:T(8,128)(2,1)S(1)} %maximum_dynamic-update-slice_fusion.12, bf16[1024,2048]{1,0:T(8,128)(2,1)S(1)} %bitcast.152), kind=kOutput, calls=%fused_computation.1 | convolution fusion | flops 2147483648 | bytes 8388608 | tf_op jit(solution)/shard_map/dot_general | solution.py:230
  86.6 2.4 %fusion.106 = (bf16[1024,1024]{0,1:T(8,128)(2,1)S(1)}, f32[1024,1024]{0,1:T(8,128)S(1)}) fusion(f32[1024,1024]{0,1:T(8,128)S(1)} %fusion, bf16[1024,1024]{0,1:T(8,128)(2,1)S(1)} %maximum_dynamic-update-slice_fusion.8, bf16[1024,2048]{1,0:T(8,128)(2,1)S(1)} %bitcast.149), kind=kOutput, calls=%fused_computation.209 | convolution fusion | flops 2149580800 | bytes 14680064 | tf_op jit(solution)/shard_map/dot_general | solution.py:230
  96.0 2.6 %convolution_convert_fusion = bf16[1024,1024]{1,0:T(8,128)(2,1)S(1)} fusion(bf16[1024,1024]{0,1:T(8,128)(2,1)S(1)} %maximum_dynamic-update-slice_fusion.12, bf16[1024,256]{0,1:T(8,128)(2,1)S(1)} %get-tuple-element.49, bf16[1024,384]{0,1:T(8,128)(2,1)S(1)} %get-tuple-element.15, bf16[1024,384]{0,1:T(8,128)(2,1)S(1)} %get-tuple-element.14), kind=kOutput, calls=%fused_computation.11 | convolution fusion | flops 2154823680 | bytes 6291456 | tf_op jit(solution)/shard_map/dot_general | solution.py:234
  99.0 3.8 %collective-permute-done = bf16[1024,1024]{1,0:T(8,128)(2,1)S(1)} collective-permute-done((bf16[1024,1024]{1,0:T(8,128)(2,1)S(1)}, bf16[1024,1024]{1,0:T(8,128)(2,1)S(1)}, u32[]{:S(2)}, u32[]{:S(2)}) %collective-permute-start) | collective-permute-done | bytes 2097184 | tf_op jit(solution)/shard_map/ppermute | solution.py:243
  102.8 3.8 %add_convert_fusion = bf16[1024,1024]{1,0:T(8,128)(2,1)} fusion(bf16[1024,1024]{1,0:T(8,128)(2,1)S(1)} %collective-permute-done, bf16[1024,1024]{0,1:T(8,128)(2,1)S(1)} %maximum_dynamic-update-slice_fusion.8, bf16[1024,256]{0,1:T(8,128)(2,1)S(1)} %get-tuple-element.49, bf16[1024,384]{0,1:T(8,128)(2,1)S(1)} %get-tuple-element.15, ...), kind=kOutput, calls=%fused_computation | convolution fusion | flops 2159017984 | bytes 8388608 | tf_op jit(solution)/shard_map/dot_general | solution.py:234
  107.5 1.4 convolution_multiply_fusion.2
  109.0 1.3 convolution_multiply_fusion.4
  110.3 1.3 convolution_multiply_fusion.3
  112.7 1.6 collective-permute-start.3
  116.2 4.9 %collective-permute-done.5 = bf16[1024,128]{0,1:T(8,128)(2,1)S(1)} collective-permute-done((bf16[1024,128]{0,1:T(8,128)(2,1)S(1)}, bf16[1024,128]{0,1:T(8,128)(2,1)S(1)}, u32[]{:S(2)}, u32[]{:S(2)}) %collective-permute-start.5) | collective-permute-done | bytes 262176 | tf_op jit(solution)/shard_map/ppermute | solution.py:248
  121.1 2.3 %convolution_multiply_fusion.1 = f32[128,512]{1,0:T(8,128)} fusion(bf16[1024,2048]{1,0:T(8,128)(2,1)} %bitcast.147, s32[]{:T(128)S(6)} %select_n.44, f32[1024,64]{0,1:T(8,128)S(1)} %broadcast_in_dim.45, f32[1024,64]{0,1:T(8,128)S(1)} %broadcast_in_dim.44, bf16[1024,128]{0,1:T(8,128)(2,1)S(1)} %collective-permute-done.5, ...), kind=kOutput, calls=%fused_computation.26 | convolution fusion | flops 135331840 | bytes 2359300 | tf_op jit(solution)/shard_map/dot_general | solution.py:238
  123.4 8.4 %collective-permute-done.3 = bf16[1024,256]{0,1:T(8,128)(2,1)S(1)} collective-permute-done((bf16[1024,256]{0,1:T(8,128)(2,1)S(1)}, bf16[1024,256]{0,1:T(8,128)(2,1)S(1)}, u32[]{:S(2)}, u32[]{:S(2)}) %collective-permute-start.3) | collective-permute-done | bytes 524320 | tf_op jit(solution)/shard_map/ppermute | solution.py:248
  131.8 1.7 convolution_multiply_fusion
  133.4 40.6 %reduce-scatter.2.cloned.1.call-done = bf16[128,1024]{1,0:T(8,128)(2,1)} async-done(((bf16[1024,1024]{1,0:T(8,128)(2,1)}), bf16[128,1024]{1,0:T(8,128)(2,1)}) %reduce-scatter.2.cloned.1.call-update) | async-done | bytes 262160 | tf_op jit(solution)/shard_map/reduce_scatter | solution.py:529
  174.9 1.5 collective-permute-start.1
  177.3 2.7 %collective-permute-done.1 = bf16[128,512]{1,0:T(8,128)(2,1)S(1)} collective-permute-done((bf16[128,512]{1,0:T(8,128)(2,1)S(1)}, bf16[128,512]{1,0:T(8,128)(2,1)S(1)}, u32[]{:S(2)}, u32[]{:S(2)}) %collective-permute-start.1) | collective-permute-done | bytes 131104 | tf_op jit(solution)/shard_map/ppermute | solution.py:248
  180.0 1.6 add_convert_fusion.6
  (99 shorter events, 22.8 us)
Async XLA Ops:
  7.2 6.9 %copy-start.13 = (bf16[2,64,2048]{2,1,0:T(8,128)(2,1)S(1)}, bf16[2,64,2048]{2,1,0:T(8,128)(2,1)}, u32[]{:S(2)}) copy-start(bf16[2,64,2048]{2,1,0:T(8,128)(2,1)} %param.25) | copy-start | bytes 1572868
  7.2 7.8 %copy-start.8 = (bf16[2,2048,192]{1,2,0:T(8,128)(2,1)S(1)}, bf16[2,2048,192]{1,2,0:T(8,128)(2,1)}, u32[]{:S(2)}) copy-start(bf16[2,2048,192]{1,2,0:T(8,128)(2,1)} %param.17) | copy-start | bytes 4718596
  7.2 166.8 %reduce-scatter.2.cloned.1.call-start = ((), (), s32[]{:S(2)}) async-start(), calls=%async_computation.1 | async-start | bytes 2359296 | tf_op jit(solution)/shard_map/reduce_scatter | solution.py:529
  14.1 2.1 %copy-start.9 = (bf16[2,2048,192]{1,2,0:T(8,128)(2,1)S(1)}, bf16[2,2048,192]{1,2,0:T(8,128)(2,1)}, u32[]{:S(2)}) copy-start(bf16[2,2048,192]{1,2,0:T(8,128)(2,1)} %param.18) | copy-start | bytes 4718596
  16.2 1.4 copy-start.10
  17.6 1.0 copy-start.3
  74.6 2.0 %copy-start = (bf16[8,128,2048]{2,1,0:T(8,128)(2,1)}, bf16[8,128,2048]{2,1,0:T(8,128)(2,1)S(1)}, u32[]{:S(2)}) copy-start(bf16[8,128,2048]{2,1,0:T(8,128)(2,1)S(1)} %get-tuple-element.11) | copy-start | bytes 12582916
  76.6 2.0 %copy-start.4 = (bf16[8,128,2048]{2,1,0:T(8,128)(2,1)}, bf16[8,128,2048]{2,1,0:T(8,128)(2,1)S(1)}, u32[]{:S(2)}) copy-start(bf16[8,128,2048]{2,1,0:T(8,128)(2,1)S(1)} %get-tuple-element.12) | copy-start | bytes 12582916
  78.6 2.4 %copy-start.11 = (bf16[1,64,2048]{2,1,0:T(8,128)(2,1)S(1)}, bf16[1,64,2048]{2,1,0:T(8,128)(2,1)}, u32[]{:S(2)}) copy-start(bf16[1,64,2048]{2,1,0:T(8,128)(2,1)} %get-tuple-element.50) | copy-start | bytes 786436
  78.7 2.4 %copy-start.12 = (bf16[1,64,2048]{2,1,0:T(8,128)(2,1)S(1)}, bf16[1,64,2048]{2,1,0:T(8,128)(2,1)}, u32[]{:S(2)}) copy-start(bf16[1,64,2048]{2,1,0:T(8,128)(2,1)} %get-tuple-element.51) | copy-start | bytes 786436
  78.7 2.5 %copy-start.6 = (bf16[1,2048,192]{1,2,0:T(8,128)(2,1)S(1)}, bf16[1,2048,192]{1,2,0:T(8,128)(2,1)}, u32[]{:S(2)}) copy-start(bf16[1,2048,192]{1,2,0:T(8,128)(2,1)} %get-tuple-element.20) | copy-start | bytes 2359300
  78.7 2.5 %copy-start.7 = (bf16[1,2048,192]{1,2,0:T(8,128)(2,1)S(1)}, bf16[1,2048,192]{1,2,0:T(8,128)(2,1)}, u32[]{:S(2)}) copy-start(bf16[1,2048,192]{1,2,0:T(8,128)(2,1)} %get-tuple-element.21) | copy-start | bytes 2359300
  81.8 2.2 %copy-start.5 = (bf16[8,128,2048]{2,1,0:T(8,128)(2,1)S(1)}, bf16[8,128,2048]{2,1,0:T(8,128)(2,1)}, u32[]{:S(2)}) copy-start(bf16[8,128,2048]{2,1,0:T(8,128)(2,1)} %copy-done.4) | copy-start | bytes 12582916
  84.0 2.6 %copy-start.1 = (bf16[8,128,2048]{2,1,0:T(8,128)(2,1)S(1)}, bf16[8,128,2048]{2,1,0:T(8,128)(2,1)}, u32[]{:S(2)}) copy-start(bf16[8,128,2048]{2,1,0:T(8,128)(2,1)} %copy-done) | copy-start | bytes 12582916
  89.0 4.3 %copy-start.15 = (bf16[1024,1024]{0,1:T(8,128)(2,1)}, bf16[1024,1024]{0,1:T(8,128)(2,1)S(1)}, u32[]{:S(2)}) copy-start(bf16[1024,1024]{0,1:T(8,128)(2,1)S(1)} %get-tuple-element.94) | copy-start | bytes 6291460
  92.0 1.3 copy-start.14
  92.2 1.1 copy-start.16
  92.2 1.1 copy-start.17
  98.5 4.3 %collective-permute-start = (bf16[1024,1024]{1,0:T(8,128)(2,1)S(1)}, bf16[1024,1024]{1,0:T(8,128)(2,1)S(1)}, u32[]{:S(2)}, u32[]{:S(2)}) collective-permute-start(bf16[1024,1024]{1,0:T(8,128)(2,1)S(1)} %convolution_convert_fusion), channel_id=1, source_target_pairs={{0,1},{1,0},{2,3},{3,2},{4,5},{5,4},{6,7},{7,6},{8,9},{9,8},{10,11... | collective-permute-start | bytes 6291464 | tf_op jit(solution)/shard_map/ppermute | solution.py:243
  106.9 4.9 %collective-permute-start.4 = (bf16[1024,128]{0,1:T(8,128)(2,1)S(1)}, bf16[1024,128]{0,1:T(8,128)(2,1)S(1)}, u32[]{:S(2)}, u32[]{:S(2)}) collective-permute-start(bf16[1024,128]{0,1:T(8,128)(2,1)S(1)} %convolution_convert_fusion.1), channel_id=1, source_target_pairs={{0,1},{1,0},{2,3},{3,2},{4,5},{5,4},{6,7},{7,6},{8,9},{9,8},{10,11... | collective-permute-start | bytes 786440 | tf_op jit(solution)/shard_map/ppermute | solution.py:243
  107.3 5.2 %collective-permute-start.2 = (bf16[1024,256]{0,1:T(8,128)(2,1)}, bf16[1024,256]{0,1:T(8,128)(2,1)S(1)}, u32[]{:S(2)}, u32[]{:S(2)}) collective-permute-start(bf16[1024,256]{0,1:T(8,128)(2,1)} %get-tuple-element.48), channel_id=1, source_target_pairs={{0,1},{1,0},{2,3},{3,2},{4,5},{5,4},{6,7},{7,6},{8,9},{9,8},{10,11... | collective-permute-start | bytes 1572872 | tf_op jit(solution)/shard_map/ppermute | solution.py:243
  111.9 9.2 %collective-permute-start.5 = (bf16[1024,128]{0,1:T(8,128)(2,1)S(1)}, bf16[1024,128]{0,1:T(8,128)(2,1)S(1)}, u32[]{:S(2)}, u32[]{:S(2)}) collective-permute-start(bf16[1024,128]{0,1:T(8,128)(2,1)S(1)} %add_convert_fusion.5), channel_id=1, source_target_pairs={{0,2},{1,3},{2,0},{3,1},{4,6},{5,7},{6,4},{7,5},{8,10},{9,11},{10,... | collective-permute-start | bytes 786440 | tf_op jit(solution)/shard_map/ppermute | solution.py:248
  112.7 19.1 %collective-permute-start.3 = (bf16[1024,256]{0,1:T(8,128)(2,1)S(1)}, bf16[1024,256]{0,1:T(8,128)(2,1)S(1)}, u32[]{:S(2)}, u32[]{:S(2)}) collective-permute-start(bf16[1024,256]{0,1:T(8,128)(2,1)S(1)} %add_convert_fusion.2), channel_id=1, source_target_pairs={{0,2},{1,3},{2,0},{3,1},{4,6},{5,7},{6,4},{7,5},{8,10},{9,11},{10,... | collective-permute-start | bytes 1572872 | tf_op jit(solution)/shard_map/ppermute | solution.py:248
  174.9 5.0 %collective-permute-start.1 = (bf16[128,512]{1,0:T(8,128)(2,1)S(1)}, bf16[128,512]{1,0:T(8,128)(2,1)S(1)}, u32[]{:S(2)}, u32[]{:S(2)}) collective-permute-start(bf16[128,512]{1,0:T(8,128)(2,1)S(1)} %constant_dynamic-slice_fusion), channel_id=1, source_target_pairs={{0,2},{1,3},{2,0},{3,1},{4,6},{5,7},{6,4},{7,5},{8,10},{9,11},{10,... | collective-permute-start | bytes 393224 | tf_op jit(solution)/shard_map/ppermute | solution.py:248
  (3 other events, 2.3 us)
Sparse Core Ops, SparseCore 0:
  106.7 67.2 reduce-scatter.1
